TPU v7x, 32 devices: a whole 2x2x4 slice. The times are simulated.
32 devices in a mesh: seq: 8 (over z, x), head: 4 (over y, core).
Axes of the slice: x: 2, y: 2, z: 4, core: 2. Of those that a mesh axis runs over, the one named last changes fastest.
Arguments:
- query_in: bfloat16 [2048, 8192], P('seq', 'head'), may hold values from -1.796875 to 1.796875
- key_in: bfloat16 [2048, 8192], P('seq', 'head'), may hold values from -1.796875 to 1.796875
- value_in: bfloat16 [2048, 8192], P('seq', 'head'), may hold values from -11 to 11
- log_decay: float32 [2048, 64], P('seq', 'head'), may hold values from -1 to 0, as said below
- norm_gain: float32 [8192], P('head'), may hold values from 0.5 to 1.5
- prompt_lengths: int32 [4], replicated, may hold values from 1 to 1536, 2048 in all
- step_query: bfloat16 [4, 128, 8192], P(None, 'seq', 'head'), may hold values from -1.796875 to 1.796875
- step_key: bfloat16 [4, 128, 8192], P(None, 'seq', 'head'), may hold values from -1.796875 to 1.796875
- step_value: bfloat16 [4, 128, 8192], P(None, 'seq', 'head'), may hold values from -6 to 6
- step_decay: float32 [4, 128, 64], P(None, 'seq', 'head'), may hold values from -0.3 to -0.01
- row_prompt: int32 [128], P('seq'), may hold values from 0 to 3
Outputs:
- attn_out: bfloat16 [2048, 8192], P('seq', 'head')
- decode_out: bfloat16 [4, 128, 8192], P(None, 'seq', 'head')
Inputs may be any that keep to these rules, and one draw needn't show every extreme that they name: `log_decay`: Negative; per head and token.
All inputs are finite; a program needn't handle non-finite values.
Results may differ from a plain program's by a relative error of at most 0.0056.
Values sent between devices are 32-bit elements; how exact they have to be, the bound alone decides.
A program may use at most 64 MiB of HBM per device.

v0:
```python
import jax
import jax.numpy as jnp
from jax import lax
from jax.sharding import PartitionSpec as P

HEAD_COUNT = 64
HDIM = 128
BLOCK = 256
PROMPTS = 4
EPSILON = 1e-06


def carried_in(part, axis, combine, identity):
    place = lax.axis_index(axis)
    gathered = jax.tree.map(lambda a: lax.all_gather(a, axis), part)
    state = jax.tree.map(lambda a, e: jnp.zeros_like(a) + jnp.asarray(e, a.dtype), part, identity)

    def one(step, state):
        return combine(
            state, jax.tree.map(lambda a: lax.dynamic_index_in_dim(a, step, 0, False), gathered)
        )

    return lax.fori_loop(0, place, one, state)


def segment_ids(prompt_lengths, positions):
    boundary = jnp.cumsum(prompt_lengths)
    return jnp.sum((positions[:, None] >= boundary[None, :]).astype(jnp.int32), axis=1)


def combine_pairs(earlier, later):
    return (earlier[0] * later[0], later[0][:, None, None] * earlier[1] + later[1])


def local(
    query_in,
    key_in,
    value_in,
    log_decay,
    norm_gain,
    prompt_lengths,
    step_query,
    step_key,
    step_value,
    step_decay,
    row_prompt,
):
    tok_count = query_in.shape[0]
    heads_here = log_decay.shape[1]
    nblocks = tok_count // BLOCK
    first = lax.axis_index("seq") * tok_count
    positions = first + jnp.arange(tok_count, dtype=jnp.int32)
    segs = segment_ids(prompt_lengths, positions)
    seg_entry = jnp.where(first > 0, segment_ids(prompt_lengths, (first - 1)[None])[0], -1)
    shape4 = (nblocks, BLOCK, heads_here, HDIM)
    queries = query_in.reshape(shape4)
    keys_blk = key_in.reshape(shape4)
    values_blk = value_in.reshape(shape4)
    cumul = jnp.cumsum(log_decay.reshape(nblocks, BLOCK, heads_here), axis=1)
    seg_blocks = segs.reshape(nblocks, BLOCK)
    seg_front = jnp.concatenate([seg_entry[None], seg_blocks[:-1, -1]])
    causal = jnp.arange(BLOCK)[:, None] >= jnp.arange(BLOCK)[None, :]
    linked = (causal[None] & (seg_blocks[:, :, None] == seg_blocks[:, None, :]))[:, None]
    cum_heads = jnp.transpose(cumul, (0, 2, 1))
    spread = cum_heads[:, :, :, None] - cum_heads[:, :, None, :]
    factor = jnp.where(linked, jnp.exp(jnp.where(linked, spread, 0.0)), 0.0)
    scores = jnp.einsum("nthd,nshd->nhts", queries, keys_blk, preferred_element_type=jnp.float32)
    weights = (scores * factor).astype(jnp.bfloat16)
    inner = jnp.einsum("nhts,nshd->nthd", weights, values_blk, preferred_element_type=jnp.float32)
    keep = (
        jnp.exp(cumul[:, -1:, :] - cumul)
        * (seg_blocks == seg_blocks[:, -1:]).astype(jnp.float32)[:, :, None]
    )
    keyed = (keys_blk.astype(jnp.float32) * keep[..., None]).astype(jnp.bfloat16)
    updates = jnp.einsum("nshd,nshe->nhde", keyed, values_blk, preferred_element_type=jnp.float32)
    onward = (
        jnp.exp(cumul[:, -1, :]) * (seg_blocks[:, -1] == seg_front).astype(jnp.float32)[:, None]
    )
    local_states = [jnp.zeros((heads_here, HDIM, HDIM), jnp.float32)]
    growth = [jnp.ones((heads_here,), jnp.float32)]
    blk_index = 0
    local_states.append(onward[blk_index][:, None, None] * local_states[-1] + updates[blk_index])
    growth.append(onward[blk_index] * growth[-1])
    summary = (growth[-1], local_states[-1])
    identity = (
        jnp.ones((heads_here,), jnp.float32),
        jnp.zeros((heads_here, HDIM, HDIM), jnp.float32),
    )
    entry = carried_in(summary, "seq", combine_pairs, identity)
    entry_state = entry[1]
    start_states = jnp.stack([local_states[0] + growth[0][:, None, None] * entry_state])
    state_half = start_states.astype(jnp.bfloat16)
    carried = jnp.exp(cumul) * (seg_blocks == seg_front[:, None]).astype(jnp.float32)[:, :, None]
    outer = (
        jnp.einsum("nthd,nhde->nthe", queries, state_half, preferred_element_type=jnp.float32)
        * carried[..., None]
    )
    mixed = (inner + outer).reshape(tok_count, heads_here * HDIM)
    squares = lax.psum(jnp.sum(mixed * mixed, axis=1), "head")
    scale = lax.rsqrt(squares / (HEAD_COUNT * HDIM) + EPSILON)
    attn_out = (mixed * scale[:, None] * norm_gain[None, :]).astype(jnp.bfloat16)
    boundary = jnp.cumsum(prompt_lengths)

    def prompt_end(prompt):
        last_tok = boundary[prompt] - 1
        local_tok = last_tok - first
        owned = (local_tok >= 0) & (local_tok < tok_count)
        safe_tok = jnp.clip(local_tok, 0, tok_count - 1)
        blk_index = safe_tok // BLOCK
        offset = safe_tok - blk_index * BLOCK
        cum_blk = cumul[blk_index]
        reached = cum_blk[offset]
        taken = (jnp.arange(BLOCK) <= offset) & (seg_blocks[blk_index] == prompt)
        keep_end = (
            jnp.exp(jnp.where(taken[:, None], reached[None, :] - cum_blk, 0.0))
            * taken.astype(jnp.float32)[:, None]
        )
        tailed = (keys_blk[blk_index].astype(jnp.float32) * keep_end[:, :, None]).astype(
            jnp.bfloat16
        )
        part = jnp.einsum(
            "shd,she->hde", tailed, values_blk[blk_index], preferred_element_type=jnp.float32
        )
        lead = jnp.exp(reached) * (seg_front[blk_index] == prompt).astype(jnp.float32)
        total = lead[:, None, None] * start_states[blk_index] + part
        return total * owned.astype(jnp.float32)

    candidates = lax.map(prompt_end, jnp.arange(PROMPTS, dtype=jnp.int32))
    prompt_state = lax.psum(candidates, "seq")
    rows_here = row_prompt.shape[0]
    row_states = jnp.take(prompt_state, row_prompt, axis=0)
    results = []
    for section in range(step_query.shape[0]):
        query_now = step_query[section].astype(jnp.float32).reshape(rows_here, heads_here, HDIM)
        key_now = step_key[section].astype(jnp.float32).reshape(rows_here, heads_here, HDIM)
        value_now = step_value[section].astype(jnp.float32).reshape(rows_here, heads_here, HDIM)
        row_states = (
            jnp.exp(step_decay[section])[:, :, None, None] * row_states
            + key_now[:, :, :, None] * value_now[:, :, None, :]
        )
        results.append(
            jnp.einsum(
                "rhd,rhde->rhe", query_now, row_states, precision=lax.Precision.HIGHEST
            ).reshape(rows_here, heads_here * HDIM)
        )
    decoded = jnp.stack(results)
    step_squares = lax.psum(jnp.sum(decoded * decoded, axis=2), "head")
    step_scale = lax.rsqrt(step_squares / (HEAD_COUNT * HDIM) + EPSILON)
    decode_out = (decoded * step_scale[:, :, None] * norm_gain[None, None, :]).astype(jnp.bfloat16)
    return (attn_out, decode_out)


def solution(mesh):
    in_specs = (
        P("seq", "head"),
        P("seq", "head"),
        P("seq", "head"),
        P("seq", "head"),
        P("head"),
        P(),
        P(None, "seq", "head"),
        P(None, "seq", "head"),
        P(None, "seq", "head"),
        P(None, "seq", "head"),
        P("seq"),
    )
    out_specs = (P("seq", "head"), P(None, "seq", "head"))
    return jax.shard_map(local, mesh=mesh, in_specs=in_specs, out_specs=out_specs, check_vma=False)
```

profile of v0, /device:TPU:0, one launch (start us, length us, event | category | flops | bytes accessed | tf_op | source)
XLA Modules:
  0.0 465.3 jit_solution(464305001508278530)
XLA Ops:
  14.8 2.6 convolution_add_fusion.1
  20.5 22.7 %all-gather = f32[8,1,16]{2,1,0:T(1,128)S(1)} all-gather(f32[1,1,16]{2,1,0:T(1,128)S(1)} %get-tuple-element.344), channel_id=2, replica_groups=mesh['seq'=8,'head'=4] {'seq'}, dimensions={0}, use_global_device_ids=true | all-gather | bytes 576 | tf_op jit(solution)/shard_map/all_gather | solution.py:15
  43.2 101.7 %all-gather.4.cloned.1.call-done = f32[128,128,128]{2,1,0:T(8,128)} async-done(((f32[16,128,128]{2,1,0:T(8,128)}), f32[128,128,128]{2,1,0:T(8,128)}) %all-gather.4.cloned.1.call-update) | async-done | bytes 8388624 | tf_op jit(solution)/shard_map/all_gather | solution.py:15
  145.0 32.4 %while.26 = (s32[]{:T(128)}, f32[4,16,128,128]{3,2,1,0:T(8,128)}, s32[4]{0:T(128)S(1)}, s32[4]{0:T(128)S(1)}, s32[]{:T(128)}, /*index=5*/f32[1,256,16]{1,2,0:T(8...) while((s32[]{:T(128)}, f32[4,16,128,128]{3,2,1,0:T(8,128)}, ...), condition=%wide.region_10.11_spmd, body=%wide.region_9.10_spmd.sunk | while | flops 136590384 | bytes 4248923 | solution.py:128
  150.4 2.7 fusion.78
  158.6 2.6 fusion.78
  166.7 2.7 fusion.78
  174.7 2.6 fusion.78
  177.4 1.6 convert_bitcast_fusion.1
  179.7 1.7 convert_bitcast_fusion
  183.4 1.6 fusion.54
  186.6 1.6 reshape.534
  191.4 1.6 reshape.538
  198.2 4.4 fusion.36
  202.6 4.1 multiply_reduce_fusion
  206.7 1.9 copy.131
  208.7 133.8 %all-reduce.3.cloned.1.call-done = f32[4,16,128,128]{3,2,1,0:T(8,128)} async-done(((f32[4,16,128,128]{3,2,1,0:T(8,128)}), f32[4,16,128,128]{3,2,1,0:T(8,128)}) %all-reduce.3.cloned.1.call-update) | async-done | bytes 4194320 | tf_op jit(solution)/shard_map/psum | solution.py:129
  342.5 10.0 %gather_fusion = f32[16,16,128,128]{3,2,1,0:T(8,128)} fusion(f32[4,16,128,128]{3,2,1,0:T(8,128)} %all-reduce.3.cloned.1.call-done, s32[1024]{0:T(1024)S(1)} %pad_clamp_fusion), kind=kCustom, calls=%fused_computation | custom fusion | bytes 33554496 | tf_op jit(solution)/shard_map/jit(_take)/gather | solution.py:131
  352.5 17.9 %fusion.15 = f32[16,16,1,128]{3,2,1,0:T(1,128)} fusion(bf16[16,16,128,1]{2,3,1,0:T(2,128)(2,1)S(1)} %copy-done.3, f32[16,16,128]{2,1,0:T(8,128)} %bitcast.215, f32[16,16,128]{2,1,0:T(8,128)} %bitcast.212, f32[16,16]{1,0:T(8,128)S(1)} %get-tuple-element.346, f32[16,16,128,128]{3,2,1,0:T(8,128)} %gather_fusion, f32[16,16,128]{2,1,0:T(8,128)} %bitcast.208, ...), kind=kOutput, calls=%fused_computation.28 | convolution fusion | flops 79691776 | bytes 17500176 | tf_op jit(solution)/shard_map/rhd,rhde->rhe/dot_general | solution.py:142
  371.4 13.4 %fusion.52 = f32[16,16,1,128]{3,2,1,0:T(1,128)} fusion(bf16[16,16,128,1]{2,3,1,0:T(2,128)(2,1)S(1)} %copy-done.2, f32[16,16,128,128]{3,2,1,0:T(8,128)} %gather_fusion, f32[16,16,128]{2,1,0:T(8,128)} %bitcast.209, f32[16,16,128]{2,1,0:T(8,128)S(1)} %bitcast.207, f32[16,16]{1,0:T(8,128)} %get-tuple-element.347, pred[16]{0:T(512)(128)(4,1)} %compare_and_fusion.1), kind=kOutput, calls=%fused_computation.108 | convolution fusion | flops 67108864 | bytes 17237008 | tf_op jit(solution)/shard_map/rhd,rhde->rhe/dot_general | solution.py:142
  386.4 22.6 %fusion.16 = f32[16,16,1,128]{3,2,1,0:T(1,128)} fusion(bf16[16,16,128,1]{2,3,1,0:T(2,128)(2,1)} %reshape.538, f32[16,16,128]{2,1,0:T(8,128)} %bitcast.220, f32[16,16,128]{2,1,0:T(8,128)} %bitcast.218, f32[16,16]{1,0:T(8,128)} %get-tuple-element.348, f32[16,16,128]{2,1,0:T(8,128)} %bitcast.216, f32[16,16,128]{2,1,0:T(8,128)} %bitcast.213, ...), kind=kOutput, calls=%fused_computation.29 | convolution fusion | flops 92274688 | bytes 17763344 | tf_op jit(solution)/shard_map/rhd,rhde->rhe/dot_general | solution.py:142
  409.9 34.9 %fusion.11 = f32[16,16,1,128]{3,2,1,0:T(1,128)} fusion(bf16[16,16,128,1]{2,3,1,0:T(2,128)(2,1)S(1)} %copy-done.1, f32[16,16,128]{2,1,0:T(8,128)} %bitcast.223, f32[16,16,128]{2,1,0:T(8,128)} %bitcast.222, f32[16,16]{1,0:T(8,128)S(1)} %get-tuple-element.345, f32[16,16,128]{2,1,0:T(8,128)} %bitcast.221, f32[16,16,128]{2,1,0:T(8,128)} %bitcast.219, ...), kind=kOutput, calls=%fused_computation.21 | convolution fusion | flops 104857600 | bytes 18026512 | tf_op jit(solution)/shard_map/rhd,rhde->rhe/dot_general | solution.py:142
  448.9 6.4 %all-reduce = (f32[256]{0:T(256)S(1)}, f32[4,16]{1,0:T(4,128)S(1)}) all-reduce(f32[256]{0:T(256)} %get-tuple-element.351, f32[4,16]{1,0:T(4,128)S(1)} %multiply_reduce_fusion.1), channel_id=1, replica_groups=mesh['seq'=8,'head'=4] {'head'}, use_global_device_ids=true, to_apply=%region_8.9 | all-reduce | flops 320 | bytes 2560 | tf_op jit(solution)/shard_map/psum | solution.py:99
  455.4 1.9 multiply_convert_fusion.4
  (106 shorter events, 39.3 us)
Async XLA Ops:
  7.2 191.1 %copy-start = (bf16[256,2048]{1,0:T(8,128)(2,1)S(1)}, bf16[256,2048]{1,0:T(8,128)(2,1)}, u32[]{:S(2)}) copy-start(bf16[256,2048]{1,0:T(8,128)(2,1)} %param.15) | copy-start | bytes 3145732
  7.2 137.7 %all-gather.4.cloned.1.call-start = ((), (), s32[]{:S(2)}) async-start(), calls=%async_computation.1 | async-start | bytes 9437184 | tf_op jit(solution)/shard_map/all_gather | solution.py:15
  17.5 325.0 %all-reduce.3.cloned.1.call-start = ((), (), s32[]{:S(2)}) async-start(), calls=%async_computation | async-start | bytes 8388608 | tf_op jit(solution)/shard_map/psum | solution.py:129
  145.0 51.2 %copy-start.7 = (s32[16]{0:T(128)S(1)}, s32[16]{0:T(128)}, u32[]{:S(2)}) copy-start(s32[16]{0:T(128)} %param.25) | copy-start | bytes 196
  198.1 188.2 %copy-start.6 = (f32[16,16]{1,0:T(8,128)}, f32[16,16]{1,0:T(8,128)S(1)}, u32[]{:S(2)}) copy-start(f32[16,16]{1,0:T(8,128)S(1)} %get-tuple-element.346) | copy-start | bytes 3076
  208.6 143.9 %copy-start.3 = (bf16[16,16,128,1]{2,3,1,0:T(2,128)(2,1)S(1)}, bf16[16,16,128,1]{2,3,1,0:T(2,128)(2,1)}, u32[]{:S(2)}) copy-start(bf16[16,16,128,1]{2,3,1,0:T(2,128)(2,1)} %reshape.536) | copy-start | bytes 196612
  208.7 143.8 %copy-start.4 = (f32[2,8,16,128]{3,2,1,0:T(8,128)S(1)}, f32[2,8,16,128]{3,2,1,0:T(8,128)}, u32[]{:S(2)}) copy-start(f32[2,8,16,128]{3,2,1,0:T(8,128)} %copy.151) | copy-start | bytes 393220
  352.5 18.9 %copy-start.2 = (bf16[16,16,128,1]{2,3,1,0:T(2,128)(2,1)S(1)}, bf16[16,16,128,1]{2,3,1,0:T(2,128)(2,1)}, u32[]{:S(2)}) copy-start(bf16[16,16,128,1]{2,3,1,0:T(2,128)(2,1)} %reshape.534) | copy-start | bytes 196612
  386.4 23.6 %copy-start.1 = (bf16[16,16,128,1]{2,3,1,0:T(2,128)(2,1)S(1)}, bf16[16,16,128,1]{2,3,1,0:T(2,128)(2,1)}, u32[]{:S(2)}) copy-start(bf16[16,16,128,1]{2,3,1,0:T(2,128)(2,1)} %reshape.540) | copy-start | bytes 196612
  409.9 45.4 %copy-start.5 = (f32[2048]{0:T(1024)S(1)}, f32[2048]{0:T(1024)}, u32[]{:S(2)}) copy-start(f32[2048]{0:T(1024)} %param.19) | copy-start | bytes 24580
Sparse Core Ops, SparseCore 0:
  17.6 127.2 all-gather.3
  177.5 164.8 all-reduce.2
where the time goes:
time: 467 us; the launch traced here: 465 us
  waiting for transfers between devices  235 us (50%)
  matrix products  111 us (24%)
  local copies, waits for them, and re-layouts  46.8 us (10%)
  blocking collectives  29.1 us (6%)
  between operations  15.6 us (3%)
  other arithmetic  14.4 us (3%)
  loops' own time  13.2 us (3%)
    psum x1, waiting for transfers between devices, local(): prompt_state = lax.psum(candidates, 'seq')  134 us
    all_gather x1, waiting for transfers between devices, carried_in(): gathered = jax.tree.map(lambda a: lax.all_gather(a, axis), part)  102 us
    dot_general x4, matrix products, local(): jnp.einsum('rhd,rhde->rhe', query_now, row_states, precision=lax.Precisio...  88.8 us
    all_gather x1, blocking collectives, carried_in(): gathered = jax.tree.map(lambda a: lax.all_gather(a, axis), part)  22.7 us
    another operation x1, loops' own time, local(): candidates = lax.map(prompt_end, jnp.arange(PROMPTS, dtype=jnp.int32))  13.2 us
    unnamed x28, local copies, waits for them, and re-layouts  11.6 us
    dot_general x4, matrix products, prompt_end(): jnp.einsum('shd,she->hde', tailed, values_blk[blk_index], preferred_eleme...  10.7 us
    gather x1, local copies, waits for them, and re-layouts, local(): row_states = jnp.take(prompt_state, row_prompt, axis=0)  10 us
  transfers between devices with their start and end apart: 2, of which 2 were waited for; matrix products, arithmetic and copies ran while one was open for 7% of the time, Pallas kernels for 0%

commit v1 on v0

--- a/solution.py
+++ b/solution.py
@@ -126,7 +126,7 @@
         return total * owned.astype(jnp.float32)
 
     candidates = lax.map(prompt_end, jnp.arange(PROMPTS, dtype=jnp.int32))
-    prompt_state = lax.psum(candidates, "seq")
+    prompt_state = jnp.sum(lax.all_gather(candidates, "seq"), axis=0)
     rows_here = row_prompt.shape[0]
     row_states = jnp.take(prompt_state, row_prompt, axis=0)
     results = []

time: 467 us -> 959 us (2.05)
  waiting for transfers between devices: 235 us -> 717 us
  other arithmetic: 14.4 us -> 28 us
    all_gather x0 -> x1, waiting for transfers between devices: none -> 616 us  [local(): prompt_state = jnp.sum(lax.all_gather(candidates, 'seq'), axis=0)]
    psum x1 -> x0, waiting for transfers between devices: 134 us -> none  [local(): prompt_state = lax.psum(candidates, 'seq')]
    reduce_sum x0 -> x1, other arithmetic: none -> 14.2 us  [local(): prompt_state = jnp.sum(lax.all_gather(candidates, 'seq'), axis=0)]
  transfers between devices with their start and end apart: 2 -> 2, of which waited for: 2 -> 2; matrix products, arithmetic and copies ran while one was open for 7% -> 3% of each run, Pallas kernels for 0% -> 0%
where the time goes in v1:
time: 959 us; the launch traced here: 957 us
  waiting for transfers between devices  717 us (75%)
  matrix products  109 us (11%)
  local copies, waits for them, and re-layouts  44.2 us (5%)
  blocking collectives  29.1 us (3%)
  other arithmetic  28 us (3%)
  between operations  15.7 us (2%)
  loops' own time  13.2 us (1%)
    all_gather x1, waiting for transfers between devices, local(): prompt_state = jnp.sum(lax.all_gather(candidates, 'seq'), axis=0)  616 us
    all_gather x1, waiting for transfers between devices, carried_in(): gathered = jax.tree.map(lambda a: lax.all_gather(a, axis), part)  102 us
    dot_general x4, matrix products, local(): jnp.einsum('rhd,rhde->rhe', query_now, row_states, precision=lax.Precisio...  87.7 us
    all_gather x1, blocking collectives, carried_in(): gathered = jax.tree.map(lambda a: lax.all_gather(a, axis), part)  22.7 us
  transfers between devices with their start and end apart: 2, of which 2 were waited for; matrix products, arithmetic and copies ran while one was open for 3% of the time, Pallas kernels for 0%

profile of v1, /device:TPU:0, one launch (start us, length us, event | category | flops | bytes accessed | tf_op | source)
XLA Modules:
  0.0 957.2 jit_solution(7456009112177897565)
XLA Ops:
  14.9 2.6 convolution_add_fusion.1
  20.6 22.7 %all-gather = f32[8,1,16]{2,1,0:T(1,128)S(1)} all-gather(f32[1,1,16]{2,1,0:T(1,128)S(1)} %get-tuple-element.344), channel_id=2, replica_groups=mesh['seq'=8,'head'=4] {'seq'}, dimensions={0}, use_global_device_ids=true | all-gather | bytes 576 | tf_op jit(solution)/shard_map/all_gather | solution.py:15
  43.3 101.6 %all-gather.6.cloned.1.call-done = f32[128,128,128]{2,1,0:T(8,128)} async-done(((f32[16,128,128]{2,1,0:T(8,128)}), f32[128,128,128]{2,1,0:T(8,128)}) %all-gather.6.cloned.1.call-update) | async-done | bytes 8388624 | tf_op jit(solution)/shard_map/all_gather | solution.py:15
  145.1 32.4 %while.26 = (s32[]{:T(128)}, f32[4,16,128,128]{3,2,1,0:T(8,128)}, s32[4]{0:T(128)S(1)}, s32[4]{0:T(128)S(1)}, s32[]{:T(128)}, /*index=5*/f32[1,256,16]{1,2,0:T(8...) while((s32[]{:T(128)}, f32[4,16,128,128]{3,2,1,0:T(8,128)}, ...), condition=%wide.region_10.11_spmd, body=%wide.region_9.10_spmd.sunk | while | flops 136590384 | bytes 4248923 | solution.py:128
  150.5 2.7 fusion.78
  158.6 2.7 fusion.78
  166.7 2.7 fusion.78
  174.8 2.7 fusion.78
  177.5 1.6 convert_bitcast_fusion.1
  179.8 1.7 convert_bitcast_fusion
  183.5 1.6 fusion.54
  186.7 1.6 reshape.535
  197.8 4.3 fusion.36
  202.1 4.0 multiply_reduce_fusion
  206.1 1.9 copy.131
  208.0 615.8 %all-gather.8.cloned.1.call-done = f32[32,16,128,128]{3,2,1,0:T(8,128)} async-done(((f32[4,16,128,128]{3,2,1,0:T(8,128)}), f32[32,16,128,128]{3,2,1,0:T(8,128)}) %all-gather.8.cloned.1.call-update) | async-done | bytes 33554448 | tf_op jit(solution)/shard_map/all_gather | solution.py:129
  823.8 14.2 %reduce_sum.48 = f32[4,16,128,128]{3,2,1,0:T(8,128)} reduce(f32[8,4,16,128,128]{4,3,2,1,0:T(8,128)} %bitcast.198, f32[]{:T(128)} %constant.128.clone.1), dimensions={0}, to_apply=%region_11.12 | reduce | flops 7340032 | bytes 37748740 | tf_op jit(solution)/shard_map/reduce_sum | solution.py:129
  838.0 10.1 %gather_fusion = f32[16,16,128,128]{3,2,1,0:T(8,128)} fusion(f32[4,16,128,128]{3,2,1,0:T(8,128)} %reduce_sum.48, s32[1024]{0:T(1024)S(1)} %pad_clamp_fusion), kind=kCustom, calls=%fused_computation | custom fusion | bytes 33554496 | tf_op jit(solution)/shard_map/jit(_take)/gather | solution.py:131
  848.2 16.7 %fusion.15 = f32[16,16,1,128]{3,2,1,0:T(1,128)S(1)} fusion(bf16[16,16,128,1]{2,3,1,0:T(2,128)(2,1)S(1)} %copy-done.5, f32[16,16,128]{2,1,0:T(8,128)S(1)} %bitcast.218, f32[16,16,128]{2,1,0:T(8,128)S(1)} %bitcast.215, f32[16,16]{1,0:T(8,128)S(1)} %get-tuple-element.346, f32[16,16,128,128]{3,2,1,0:T(8,128)} %gather_fusion, f32[16,16,128]{2,1,0:T(8,128)S(1)} %bitcast.211, ...), kind=kOutput, calls=%fused_computation.28 | convolution fusion | flops 79691776 | bytes 17500176 | tf_op jit(solution)/shard_map/rhd,rhde->rhe/dot_general | solution.py:142
  865.0 12.7 %fusion.52 = f32[16,16,1,128]{3,2,1,0:T(1,128)S(1)} fusion(bf16[16,16,128,1]{2,3,1,0:T(2,128)(2,1)S(1)} %copy-done.3, f32[16,16,128,128]{3,2,1,0:T(8,128)} %gather_fusion, f32[16,16,128]{2,1,0:T(8,128)S(1)} %bitcast.212, f32[16,16,128]{2,1,0:T(8,128)S(1)} %bitcast.208, f32[16,16]{1,0:T(8,128)S(1)} %get-tuple-element.347, ...), kind=kOutput, calls=%fused_computation.108 | convolution fusion | flops 67108864 | bytes 17237008 | tf_op jit(solution)/shard_map/rhd,rhde->rhe/dot_general | solution.py:142
  878.5 23.2 %fusion.16 = f32[16,16,1,128]{3,2,1,0:T(1,128)S(1)} fusion(bf16[16,16,128,1]{2,3,1,0:T(2,128)(2,1)S(1)} %copy-done.4, f32[16,16,128]{2,1,0:T(8,128)S(1)} %bitcast.223, f32[16,16,128]{2,1,0:T(8,128)S(1)} %bitcast.221, f32[16,16]{1,0:T(8,128)} %get-tuple-element.348, f32[16,16,128]{2,1,0:T(8,128)S(1)} %bitcast.219, f32[16,16,128]{2,1,0:T(8,128)S(1)} %bitcast.216, ...), kind=kOutput, calls=%fused_computation.29 | convolution fusion | flops 92274688 | bytes 17763344 | tf_op jit(solution)/shard_map/rhd,rhde->rhe/dot_general | solution.py:142
  901.8 35.0 %fusion.11 = f32[16,16,1,128]{3,2,1,0:T(1,128)} fusion(bf16[16,16,128,1]{2,3,1,0:T(2,128)(2,1)S(1)} %copy-done.2, f32[16,16,128]{2,1,0:T(8,128)} %bitcast.225, f32[16,16,128]{2,1,0:T(8,128)} %bitcast.224, f32[16,16]{1,0:T(8,128)S(1)} %get-tuple-element.345, f32[16,16,128]{2,1,0:T(8,128)} %bitcast.222, f32[16,16,128]{2,1,0:T(8,128)} %bitcast.220, ...), kind=kOutput, calls=%fused_computation.21 | convolution fusion | flops 104857600 | bytes 18026512 | tf_op jit(solution)/shard_map/rhd,rhde->rhe/dot_general | solution.py:142
  940.9 6.4 all-reduce
  947.3 1.9 multiply_convert_fusion.4
  (125 shorter events, 37.8 us)
Async XLA Ops:
  7.2 190.6 %copy-start = (bf16[256,2048]{1,0:T(8,128)(2,1)S(1)}, bf16[256,2048]{1,0:T(8,128)(2,1)}, u32[]{:S(2)}) copy-start(bf16[256,2048]{1,0:T(8,128)(2,1)} %param.15) | copy-start | bytes 3145732
  7.2 137.8 %all-gather.6.cloned.1.call-start = ((), (), s32[]{:S(2)}) async-start(), calls=%async_computation | async-start | bytes 9437184 | tf_op jit(solution)/shard_map/all_gather | solution.py:15
  17.6 806.2 %all-gather.8.cloned.1.call-start = ((), (), s32[]{:S(2)}) async-start(), calls=%async_computation.1 | async-start | bytes 37748736 | tf_op jit(solution)/shard_map/all_gather | solution.py:129
  145.1 51.1 %copy-start.15 = (s32[16]{0:T(128)S(1)}, s32[16]{0:T(128)}, u32[]{:S(2)}) copy-start(s32[16]{0:T(128)} %param.25) | copy-start | bytes 196
  196.3 668.7 %copy-start.16 = (pred[16]{0:T(512)(128)(4,1)}, pred[16]{0:T(512)(128)(4,1)S(1)}, u32[]{:S(2)}) copy-start(pred[16]{0:T(512)(128)(4,1)S(1)} %compare_and_fusion.1) | copy-start | bytes 52
  197.6 667.3 %copy-start.14 = (f32[16,16]{1,0:T(8,128)}, f32[16,16]{1,0:T(8,128)S(1)}, u32[]{:S(2)}) copy-start(f32[16,16]{1,0:T(8,128)S(1)} %get-tuple-element.347) | copy-start | bytes 3076
  197.6 680.8 %copy-start.13 = (f32[16,16]{1,0:T(8,128)}, f32[16,16]{1,0:T(8,128)S(1)}, u32[]{:S(2)}) copy-start(f32[16,16]{1,0:T(8,128)S(1)} %get-tuple-element.346) | copy-start | bytes 3076
  838.0 10.1 %copy-start.5 = (bf16[16,16,128,1]{2,3,1,0:T(2,128)(2,1)S(1)}, bf16[16,16,128,1]{2,3,1,0:T(2,128)(2,1)}, u32[]{:S(2)}) copy-start(bf16[16,16,128,1]{2,3,1,0:T(2,128)(2,1)} %reshape.537) | copy-start | bytes 196612
  838.0 10.1 %copy-start.6 = (f32[2,8,16,128]{3,2,1,0:T(8,128)S(1)}, f32[2,8,16,128]{3,2,1,0:T(8,128)}, u32[]{:S(2)}) copy-start(f32[2,8,16,128]{3,2,1,0:T(8,128)} %copy.151) | copy-start | bytes 393220
  838.0 10.1 %copy-start.7 = (f32[2,8,16,128]{3,2,1,0:T(8,128)S(1)}, f32[2,8,16,128]{3,2,1,0:T(8,128)}, u32[]{:S(2)}) copy-start(f32[2,8,16,128]{3,2,1,0:T(8,128)} %copy.152) | copy-start | bytes 393220
  838.0 10.1 %copy-start.8 = (f32[2,8,16,128]{3,2,1,0:T(8,128)S(1)}, f32[2,8,16,128]{3,2,1,0:T(8,128)}, u32[]{:S(2)}) copy-start(f32[2,8,16,128]{3,2,1,0:T(8,128)} %copy.153) | copy-start | bytes 393220
  838.0 10.1 %copy-start.9 = (f32[2,8,16,128]{3,2,1,0:T(8,128)S(1)}, f32[2,8,16,128]{3,2,1,0:T(8,128)}, u32[]{:S(2)}) copy-start(f32[2,8,16,128]{3,2,1,0:T(8,128)} %copy.154) | copy-start | bytes 393220
  848.2 16.8 %copy-start.3 = (bf16[16,16,128,1]{2,3,1,0:T(2,128)(2,1)S(1)}, bf16[16,16,128,1]{2,3,1,0:T(2,128)(2,1)}, u32[]{:S(2)}) copy-start(bf16[16,16,128,1]{2,3,1,0:T(2,128)(2,1)} %reshape.535) | copy-start | bytes 196612
  864.9 13.6 %copy-start.4 = (bf16[16,16,128,1]{2,3,1,0:T(2,128)(2,1)S(1)}, bf16[16,16,128,1]{2,3,1,0:T(2,128)(2,1)}, u32[]{:S(2)}) copy-start(bf16[16,16,128,1]{2,3,1,0:T(2,128)(2,1)} %reshape.539) | copy-start | bytes 196612
  864.9 13.5 %copy-start.10 = (f32[2,8,16,128]{3,2,1,0:T(8,128)S(1)}, f32[2,8,16,128]{3,2,1,0:T(8,128)}, u32[]{:S(2)}) copy-start(f32[2,8,16,128]{3,2,1,0:T(8,128)} %copy.155) | copy-start | bytes 393220
  864.9 13.5 %copy-start.11 = (f32[2,8,16,128]{3,2,1,0:T(8,128)S(1)}, f32[2,8,16,128]{3,2,1,0:T(8,128)}, u32[]{:S(2)}) copy-start(f32[2,8,16,128]{3,2,1,0:T(8,128)} %copy.156) | copy-start | bytes 393220
  878.5 23.3 %copy-start.2 = (bf16[16,16,128,1]{2,3,1,0:T(2,128)(2,1)S(1)}, bf16[16,16,128,1]{2,3,1,0:T(2,128)(2,1)}, u32[]{:S(2)}) copy-start(bf16[16,16,128,1]{2,3,1,0:T(2,128)(2,1)} %reshape.541) | copy-start | bytes 196612
  901.8 45.5 %copy-start.12 = (f32[2048]{0:T(1024)S(1)}, f32[2048]{0:T(1024)}, u32[]{:S(2)}) copy-start(f32[2048]{0:T(1024)} %param.19) | copy-start | bytes 24580
  901.8 48.6 %copy-start.1 = (bf16[256,2048]{1,0:T(8,128)(2,1)S(1)}, bf16[256,2048]{1,0:T(8,128)(2,1)}, u32[]{:S(2)}) copy-start(bf16[256,2048]{1,0:T(8,128)(2,1)} %param.15) | copy-start | bytes 3145732
Sparse Core Ops, SparseCore 0:
  17.7 127.2 all-gather.5
  177.6 646.1 all-gather.7
